TPU v7x, 32 devices: a whole 2x2x4 slice. The times are simulated.
32 devices in a mesh: groups: 2 (over x), expert: 16 (over z, y, core).
Axes of the slice: x: 2, y: 2, z: 4, core: 2. Of those that a mesh axis runs over, the one named last changes fastest.
Arguments:
- hidden_in: bfloat16 [256, 4096], P(('groups', 'expert')), parts along dimension 0, may hold values from -6 to 6
- queries: bfloat16 [256, 4096], P(('groups', 'expert')), parts along dimension 0, may hold values from -8 to 8
- decode_key_value: bfloat16 [256, 2, 256], P(('groups', 'expert')), parts along dimension 0, may hold values from -6 to 6
- local_kv: bfloat16 [1024, 2, 16, 256], P(('groups', 'expert')), parts along dimension 0, may hold values from -8 to 8
- page_table: int32 [256, 16], P(('groups', 'expert')), parts along dimension 0, may hold values from 0 to 31
- seq_blocks: int32 [256], P(('groups', 'expert')), parts along dimension 0, may hold values from 1 to 16
- prompt_kv: bfloat16 [32, 16, 2, 16, 256], P(('groups', 'expert')), parts along dimension 0, may hold values from -8 to 8
- prompt_owner: int32 [32], P('groups'), parts along dimension 0, may hold values from 0 to 15, as said below
- prompt_pages: int32 [32], P('groups'), parts along dimension 0, may hold values from 1 to 16
- norm_gain: float32 [4096], replicated, may hold values from 0.5 to 1.5
- router: bfloat16 [4096, 8], replicated, may hold values from -0.09375 to 0.09375
- w_gate: bfloat16 [16, 4096, 384], P('expert'), may hold values from -0.09375 to 0.09375
- w_up: bfloat16 [16, 4096, 384], P('expert'), may hold values from -0.09375 to 0.09375
- w_down: bfloat16 [16, 384, 4096], P('expert'), may hold values from -0.21875 to 0.21875
- route_ids: int32 [256, 8], P(('groups', 'expert')), parts along dimension 0, may hold values from 0 to 7, as said below
Outputs:
- layer_out: bfloat16 [256, 4096], P(('groups', 'expert')), parts along dimension 0
There are 2 independent parts, one for each index of `groups`. A program takes and returns all parts, laid end to end along the dimension named above; an argument that names none is the same for every part. Nothing has to cross between parts.
Inputs may be any that keep to these rules, and one draw needn't show every extreme that they name: `prompt_owner`: each device is named by at most 2 prompts, and by exactly 2 for some of the devices. `route_ids`: each row names 8 different experts; among the rows of one device no expert is named more than 8 times, a bound that some block reaches. `page_table`: indices among the pages of the sequence's own device.
All inputs are finite; a program needn't handle non-finite values.
Results may differ from a plain program's by a relative error of at most 0.0056.
Values may be sent and summed in bfloat16 or wider, within the bound.
A program may use at most 128 MiB of HBM per device.

v0:
```python
import math

import jax
import jax.numpy as jnp
from jax import lax
from jax.sharding import PartitionSpec as P

D = 4096
QUERY_HEADS = 32
KEY_VALUE_HEADS = 2
HEAD_SIZE = 128
PAGE_TOKENS = 16
TOPK = 8
MAXB = 16
MAXP = 2


norm_eps = 1e-06
masked_score = -1e30


def partner(x, axis, apart):
    return lax.ppermute(x, axis, [(i, i ^ 1 << apart) for i in range(lax.axis_size(axis))])


def attend(rows_of_queries, rows_of_keys, rows_of_values, allowed, token_own_key, token_own_value):
    decode_tokens = rows_of_queries.shape[0]
    heads_of_queries = rows_of_queries.reshape(
        decode_tokens, KEY_VALUE_HEADS, QUERY_HEADS // KEY_VALUE_HEADS, HEAD_SIZE
    )
    heads_of_keys = rows_of_keys.reshape(decode_tokens, -1, KEY_VALUE_HEADS, HEAD_SIZE)
    heads_of_values = rows_of_values.reshape(decode_tokens, -1, KEY_VALUE_HEADS, HEAD_SIZE)
    scale_for_scores = 1.0 / math.sqrt(HEAD_SIZE)
    allowed_mask = allowed[:, None, None, :]
    scores = (
        jnp.einsum(
            "tkgd,tlkd->tkgl", heads_of_queries, heads_of_keys, preferred_element_type=jnp.float32
        )
        * scale_for_scores
    )
    scores = jnp.where(allowed_mask, scores, masked_score)
    token_own_score = (
        jnp.einsum(
            "xejp,xep->xej",
            heads_of_queries,
            token_own_key.reshape(decode_tokens, KEY_VALUE_HEADS, HEAD_SIZE),
            preferred_element_type=jnp.float32,
        )
        * scale_for_scores
    )
    peak = jnp.maximum(jnp.max(scores, -1), token_own_score)
    weights = jnp.where(allowed_mask, jnp.exp(scores - peak[..., None]), 0.0)
    own_weight = jnp.exp(token_own_score - peak)
    denominator = jnp.sum(weights, -1) + own_weight
    probs = (weights / denominator[..., None]).astype(jnp.bfloat16)
    token_own_probability = (own_weight / denominator).astype(jnp.bfloat16)
    blended_noise = jnp.einsum(
        "tkgl,tlkd->tkgd", probs, heads_of_values, preferred_element_type=jnp.float32
    )
    blended_noise = blended_noise + token_own_probability.astype(jnp.float32)[
        ..., None
    ] * token_own_value.reshape(decode_tokens, KEY_VALUE_HEADS, 1, HEAD_SIZE).astype(jnp.float32)
    return blended_noise.reshape(decode_tokens, QUERY_HEADS * HEAD_SIZE).astype(jnp.bfloat16)


def local(
    hidden_in,
    queries,
    decode_key_value,
    local_kv,
    page_table,
    seq_blocks,
    prompt_kv,
    prompt_owner,
    prompt_pages,
    norm_gain,
    router,
    w_gate,
    w_up,
    w_down,
    route_ids,
):
    devices = lax.axis_size("expert")
    position = lax.axis_index("expert")
    experts = devices // 2
    seq_dev = hidden_in.shape[0]
    key_value_width = KEY_VALUE_HEADS * HEAD_SIZE
    capacity = min(seq_dev, max(2, 2 * ((3 * seq_dev * TOPK + 2 * devices - 1) // (2 * devices))))
    half_cap = capacity // 2
    even_core = position % 2 == 0
    prompt_count = prompt_owner.shape[0]
    prompt_range = jnp.arange(prompt_count, dtype=jnp.int32)
    same_owner = prompt_owner[:, None] == prompt_owner[None, :]
    earlier = prompt_range[None, :] < prompt_range[:, None]
    arrival = jnp.sum((same_owner & earlier).astype(jnp.int32), 1)
    matching = (
        prompt_owner[None, None, :] == jnp.arange(devices, dtype=jnp.int32)[:, None, None]
    ) & (arrival[None, None, :] == jnp.arange(MAXP, dtype=jnp.int32)[None, :, None])
    chosen_prompt = jnp.sum(jnp.where(matching, prompt_range[None, None, :], 0), -1)
    occupied = jnp.any(matching, -1)
    own_picks = lax.dynamic_index_in_dim(chosen_prompt, position, 0, keepdims=False)
    own_occupied = lax.dynamic_index_in_dim(occupied, position, 0, keepdims=False)
    page_rows = prompt_kv[0]
    outgoing = jnp.take(page_rows, chosen_prompt.T.reshape(-1), axis=0).reshape(
        MAXP, devices, 2, PAGE_TOKENS, key_value_width
    )
    outgoing = jnp.where(occupied.T[:, :, None, None, None], outgoing, 0)
    arrived = lax.all_to_all(outgoing, "expert", split_axis=1, concat_axis=1, tiled=True)
    lengths = jnp.take(prompt_pages, own_picks)
    new_keys = arrived[:, :, 0].reshape(MAXP, devices * PAGE_TOKENS, key_value_width)
    new_values = arrived[:, :, 1].reshape(MAXP, devices * PAGE_TOKENS, key_value_width)
    new_allowed = (jnp.arange(devices * PAGE_TOKENS, dtype=jnp.int32) // PAGE_TOKENS)[
        None, :
    ] < lengths[:, None]
    fresh_rows = attend(
        queries[:MAXP],
        new_keys,
        new_values,
        new_allowed,
        decode_key_value[:MAXP, 0],
        decode_key_value[:MAXP, 1],
    )
    fetched = local_kv[page_table]
    old_keys = fetched[:, :, 0].reshape(seq_dev, MAXB * PAGE_TOKENS, key_value_width)
    old_values = fetched[:, :, 1].reshape(seq_dev, MAXB * PAGE_TOKENS, key_value_width)
    old_allowed = (jnp.arange(MAXB * PAGE_TOKENS, dtype=jnp.int32) // PAGE_TOKENS)[
        None, :
    ] < seq_blocks[:, None]
    old_out = attend(
        queries, old_keys, old_values, old_allowed, decode_key_value[:, 0], decode_key_value[:, 1]
    )
    new_count = jnp.sum(own_occupied.astype(jnp.int32))
    is_new = jnp.arange(MAXP, dtype=jnp.int32) < new_count
    attention = jnp.concatenate(
        [jnp.where(is_new[:, None], fresh_rows, old_out[:MAXP]), old_out[MAXP:]], 0
    )
    residual = (hidden_in.astype(jnp.float32) + attention.astype(jnp.float32)).astype(jnp.bfloat16)
    resid_wide = residual.astype(jnp.float32)
    normed = (
        resid_wide
        * lax.rsqrt(jnp.mean(resid_wide * resid_wide, -1, keepdims=True) + norm_eps)
        * norm_gain
    ).astype(jnp.bfloat16)
    logits = jnp.dot(normed, router, preferred_element_type=jnp.float32)
    expert_onehot = route_ids[:, :, None] == jnp.arange(experts, dtype=jnp.int32)[None, None, :]
    selected = jnp.sum(jnp.where(expert_onehot, logits[:, None, :], 0.0), -1)
    gate_weights = jax.nn.softmax(selected, -1)
    assigned = seq_dev * TOPK
    expert_ids = route_ids.reshape(assigned)
    chosen = (expert_ids[:, None] == jnp.arange(experts, dtype=jnp.int32)[None, :]).astype(
        jnp.int32
    )
    before = jnp.cumsum(chosen, 0) - chosen
    slot_rank = jnp.sum(before * chosen, 1)
    slot_index = expert_ids * capacity + slot_rank
    placing = slot_index[None, :] == jnp.arange(experts * capacity, dtype=jnp.int32)[:, None]
    selector = jnp.any(placing.reshape(experts * capacity, seq_dev, TOPK), -1).astype(jnp.bfloat16)
    gathered_rows = jnp.dot(selector, normed, preferred_element_type=jnp.float32).astype(
        jnp.bfloat16
    )
    outgoing_half = gathered_rows.reshape(devices, half_cap, D)
    own_half = lax.all_to_all(outgoing_half, "expert", split_axis=0, concat_axis=0, tiled=True)
    partner_half = partner(own_half, "expert", 0)
    received = jnp.where(
        even_core,
        jnp.concatenate([own_half, partner_half], 1),
        jnp.concatenate([partner_half, own_half], 1),
    )
    flattened = received.reshape(devices * capacity, D)
    gate_proj = jnp.dot(flattened, w_gate[0], preferred_element_type=jnp.float32)
    up_proj = jnp.dot(flattened, w_up[0], preferred_element_type=jnp.float32)
    activated = (jax.nn.silu(gate_proj) * up_proj).astype(jnp.bfloat16)
    partial_value = jnp.dot(activated, w_down[0], preferred_element_type=jnp.float32).reshape(
        devices, capacity, D
    )
    kept = jnp.where(even_core, partial_value[:, :half_cap], partial_value[:, half_cap:])
    handed = jnp.where(even_core, partial_value[:, half_cap:], partial_value[:, :half_cap])
    partner_part = partner(handed, "expert", 0)
    finished = (kept + partner_part).astype(jnp.bfloat16)
    returned = lax.all_to_all(finished, "expert", split_axis=0, concat_axis=0, tiled=True)
    expert_sum = returned.reshape(experts * capacity, D)
    picked = jnp.take(expert_sum, slot_index, axis=0).astype(jnp.float32).reshape(seq_dev, TOPK, D)
    expert_mix = jnp.sum(picked * gate_weights[:, :, None], 1)
    return (resid_wide + expert_mix).astype(jnp.bfloat16)


def solution(mesh):
    return jax.shard_map(
        local,
        mesh=mesh,
        in_specs=(
            P(("groups", "expert"), None),
            P(("groups", "expert"), None),
            P(("groups", "expert"), None, None),
            P(("groups", "expert"), None, None, None),
            P(("groups", "expert"), None),
            P(("groups", "expert")),
            P(("groups", "expert"), None, None, None, None),
            P("groups"),
            P("groups"),
            P(),
            P(),
            P("expert", None, None),
            P("expert", None, None),
            P("expert", None, None),
            P(("groups", "expert"), None),
        ),
        out_specs=P(("groups", "expert"), None),
        check_vma=False,
    )
```

profile of v0, /device:TPU:0, one launch (start us, length us, event | category | flops | bytes accessed | tf_op | source)
XLA Modules:
  0.0 109.9 jit_solution(15105723009639426284)
XLA Ops:
  0.0 1.0 convert_reduce_fusion
  1.0 0.7 iota_compare_fusion.4
  1.7 0.1 and_reduce_fusion
  1.8 0.1 fusion.56
  1.9 0.1 reshape.370
  2.0 2.3 %gather_fusion.1 = bf16[32,2,16,256]{3,2,1,0:T(8,128)(2,1)} fusion(bf16[16,2,16,256]{3,2,1,0:T(8,128)(2,1)} %bitcast.111, s32[1024]{0:T(1024)S(1)} %pad_clamp_fusion.2), kind=kCustom, calls=%fused_computation.1 | custom fusion | bytes 1048704 | tf_op jit(solution)/shard_map/jit(_take)/gather | solution.py:104
  4.4 1.2 %select_select_fusion = bf16[2,16,2,16,256]{4,3,2,1,0:T(8,128)(2,1)S(1)} fusion(bf16[2,16,2,16,256]{4,3,2,1,0:T(8,128)(2,1)} %bitcast.110, pred[2,16]{1,0:T(4,128)(4,1)S(1)} %compare_and_fusion.1, pred[2,16]{1,0:T(4,128)(4,1)S(1)} %bitcast.123), kind=kLoop, calls=%fused_computation.34 | loop fusion | flops 524288 | bytes 1048640 | tf_op jit(solution)/shard_map/jit(_where)/select_n | solution.py:107
  5.5 0.9 copy.48
  6.4 7.5 %all-to-all-start = ((bf16[2,16,2,16,256]{4,3,0,2,1:T(8,128)(2,1)}), bf16[2,16,2,16,256]{4,3,0,2,1:T(8,128)(2,1)}, u32[]{:S(2)}, u32[]{:S(2)}) async-start(bf16[2,16,2,16,256]{4,3,0,2,1:T(8,128)(2,1)} %copy.48), calls=%async_computation | async-start | bytes 1048576 | tf_op jit(solution)/shard_map/all_to_all | solution.py:108
  13.9 0.1 reshape.396
  14.0 3.1 %gather_fusion.2 = bf16[128,2,16,256]{3,2,1,0:T(8,128)(2,1)} fusion(bf16[32,2,16,256]{3,2,1,0:T(8,128)(2,1)} %param.18, s32[1024]{0:T(1024)S(1)} %pad_clamp_fusion.1), kind=kCustom, calls=%fused_computation.2 | custom fusion | bytes 4194816 | tf_op jit(solution)/shard_map/gather | solution.py:123
  17.1 3.0 %slice_bitcast_fusion.1 = (bf16[8,16,1,16,256]{4,3,1,0,2:T(8,128)(2,1)}, bf16[8,16,1,16,256]{4,3,1,0,2:T(8,128)(2,1)}) fusion(bf16[8,16,2,16,256]{4,3,2,1,0:T(8,128)(2,1)} %bitcast.109), kind=kLoop, calls=%fused_computation.25 | loop fusion | bytes 4194304
  20.2 2.2 %reshape_reshape_squeeze.15 = bf16[8,256,2,128]{3,2,1,0:T(2,128)(2,1)} reshape(bf16[8,16,1,16,256]{4,3,1,0,2:T(8,128)(2,1)} %get-tuple-element.10) | data formatting | bytes 2097152 | tf_op jit(solution)/shard_map/reshape;reshape;squeeze | solution.py:32
  22.4 2.2 %reshape_reshape_squeeze.14 = bf16[8,256,2,128]{3,2,1,0:T(2,128)(2,1)} reshape(bf16[8,16,1,16,256]{4,3,1,0,2:T(8,128)(2,1)} %get-tuple-element.9) | data formatting | bytes 2097152 | tf_op jit(solution)/shard_map/reshape;reshape;squeeze | solution.py:31
  24.6 0.1 broadcast_compare_fusion
  24.7 0.1 fusion.46
  24.8 0.0 copy-start.3
  24.8 1.7 %fusion.84 = (f32[8,2,16]{2,1,0:T(2,128)S(1)}, f32[8,2,16,256]{3,2,1,0:T(8,128)S(1)}) fusion(bf16[8,2,16,128]{3,0,2,1:T(8,128)(2,1)S(1)} %bitcast.127, bf16[8,256,2,128]{3,2,1,0:T(2,128)(2,1)} %reshape_reshape_squeeze.14, pred[8,256]{1,0:T(8,128)(4,1)S(1)} %broadcast_compare_fusion), kind=kOutput, calls=%fused_computation.144 | convolution fusion | flops 16973568 | bytes 1379328 | tf_op jit(solution)/shard_map/tkgd,tlkd->tkgl/dot_general | solution.py:36
  26.6 0.0 copy-start.1
  26.6 0.2 fusion.28
  26.9 0.3 fusion.14
  27.3 0.1 reshape.373
  27.3 0.1 fusion.50
  27.4 0.1 reduce_window_sum.11
  27.5 0.2 select_reduce_fusion.1
  27.7 0.1 reduce_sum.100
  27.8 0.1 fusion.54
  27.9 0.7 fusion.68
  28.7 0.6 gather_fusion
  29.3 0.7 iota_compare_fusion.6
  30.0 0.1 broadcast_compare_fusion.1
  30.1 0.1 fusion.65
  30.2 1.8 %fusion.83 = (bf16[2,16,1,16,256]{4,3,0,2,1:T(8,128)(2,1)}, bf16[2,16,1,16,256]{4,3,0,2,1:T(8,128)(2,1)S(1)}) fusion(bf16[2,16,2,16,256]{4,3,0,2,1:T(8,128)(2,1)} %all-to-all-done), kind=kLoop, calls=%fused_computation.143 | loop fusion | bytes 1048576 | tf_op jit(solution)/shard_map/slice | solution.py:110
  32.0 0.8 reshape_reshape_squeeze.13
  32.8 1.0 copy.49
  33.7 0.8 reshape_reshape_squeeze.12
  34.5 1.2 %fusion.85 = (f32[2,2,16]{2,1,0:T(2,128)S(1)}, f32[2,2,16,256]{3,2,1,0:T(8,128)S(1)}) fusion(bf16[2,2,16,128]{3,2,1,0:T(8,128)(2,1)S(1)} %bitcast.119, bf16[2,256,2,128]{3,2,1,0:T(2,128)(2,1)} %reshape_reshape_squeeze.12, pred[2,256]{1,0:T(4,128)(4,1)S(1)} %broadcast_compare_fusion.1), kind=kOutput, calls=%fused_computation.145 | convolution fusion | flops 4243392 | bytes 344832 | tf_op jit(solution)/shard_map/tkgd,tlkd->tkgl/dot_general | solution.py:36
  35.7 0.2 fusion.49
  35.9 1.2 %fusion.20 = bf16[2,2,16,128]{3,2,1,0:T(8,128)(2,1)S(1)} fusion(bf16[2,256,2,128]{3,2,1,0:T(2,128)(2,1)} %reshape_reshape_squeeze.13, f32[2,2,16,256]{3,2,1,0:T(8,128)S(1)} %get-tuple-element.22, f32[2,2,16]{2,1,0:T(2,128)S(1)} %get-tuple-element.18, f32[2,2,16]{2,1,0:T(2,128)S(1)} %multiply_maximum_fusion.1, ...), kind=kOutput, calls=%fused_computation.23 | convolution fusion | flops 4284416 | bytes 347392 | tf_op jit(solution)/shard_map/tkgl,tlkd->tkgd/dot_general | solution.py:57
  37.1 0.1 broadcast_select_fusion
  37.2 1.0 fusion.37
  38.2 1.2 %convolution_convert_fusion = bf16[64,4096]{1,0:T(8,128)(2,1)} fusion(pred[64,8]{0,1:T(8,128)(4,1)S(1)} %fusion.54, bf16[8,4096]{1,0:T(8,128)(2,1)S(1)} %get-tuple-element.8, f32[4096]{0:T(1024)S(1)} %copy-done.5, f32[8]{0:T(128)S(1)} %add_rsqrt_fusion), kind=kOutput, calls=%fused_computation.4 | convolution fusion | flops 4587520 | bytes 606752 | tf_op jit(solution)/shard_map/dot_general | solution.py:158
  39.4 2.0 %reshape.374 = bf16[16,4,4096]{2,1,0:T(4,128)(2,1)} reshape(bf16[64,4096]{1,0:T(8,128)(2,1)} %convolution_convert_fusion) | data formatting | bytes 1048576 | tf_op jit(solution)/shard_map/reshape | solution.py:161
  41.4 20.3 %all_to_all.15 = bf16[16,4,4096]{2,1,0:T(4,128)(2,1)} all-to-all(bf16[16,4,4096]{2,1,0:T(4,128)(2,1)} %reshape.374), channel_id=1, replica_groups=mesh['groups'=2,'expert'=16] {'expert'}, dimensions={0} | all-to-all | bytes 1048576 | tf_op jit(solution)/shard_map/all_to_all | solution.py:162
  61.7 0.1 collective-permute-start
  61.9 2.1 %collective-permute-done = bf16[16,4,4096]{2,1,0:T(4,128)(2,1)} collective-permute-done((bf16[16,4,4096]{2,1,0:T(4,128)(2,1)}, bf16[16,4,4096]{2,1,0:T(4,128)(2,1)}, u32[]{:S(2)}, u32[]{:S(2)}) %collective-permute-start) | collective-permute-done | bytes 524320 | tf_op jit(solution)/shard_map/ppermute | solution.py:23
  64.0 3.8 %fusion.4 = f32[128,384]{1,0:T(8,128)S(1)} fusion(bf16[1,4096,384]{2,1,0:T(8,128)(2,1)} %param.26, bf16[16,4,4096]{2,1,0:T(4,128)(2,1)} %collective-permute-done, bf16[16,4,4096]{2,1,0:T(4,128)(2,1)} %all_to_all.15, pred[]{:T(512)S(6)} %eq.103), kind=kOutput, calls=%fused_computation.9 | convolution fusion | flops 407371776 | bytes 4390913 | tf_op jit(solution)/shard_map/dot_general | solution.py:170
  67.8 5.8 %fusion = f32[16,8,4096]{2,1,0:T(8,128)} fusion(bf16[1,384,4096]{2,1,0:T(8,128)(2,1)S(1)} %copy-done, bf16[1,4096,384]{2,1,0:T(8,128)(2,1)} %param.27, f32[128,384]{1,0:T(8,128)S(1)} %fusion.4, bf16[16,4,4096]{2,1,0:T(4,128)(2,1)} %collective-permute-done, bf16[16,4,4096]{2,1,0:T(4,128)(2,1)} %all_to_all.15, pred[]{:T(512)S(6)} %eq.103), kind=kOutput, calls=%fused_computation.5 | convolution fusion | flops 810319872 | bytes 9633793 | tf_op jit(solution)/shard_map/dot_general | solution.py:173
  73.7 3.5 %slice_select_fusion = f32[16,4,4096]{2,1,0:T(4,128)} fusion(f32[16,8,4096]{2,1,0:T(8,128)} %fusion, pred[]{:T(512)S(6)} %eq.103), kind=kLoop, calls=%fused_computation.32 | loop fusion | flops 262144 | bytes 3145729 | tf_op jit(solution)/shard_map/jit(_where)/select_n | solution.py:177
  77.2 0.1 collective-permute-start.1
  77.3 0.1 mul.136
  77.4 2.8 %collective-permute-done.1 = f32[16,4,4096]{2,1,0:T(4,128)} collective-permute-done((f32[16,4,4096]{2,1,0:T(4,128)}, f32[16,4,4096]{2,1,0:T(4,128)}, u32[]{:S(2)}, u32[]{:S(2)}) %collective-permute-start.1) | collective-permute-done | bytes 1048608 | tf_op jit(solution)/shard_map/ppermute | solution.py:23
  80.2 3.8 %add_convert_fusion = bf16[16,4,4096]{2,1,0:T(4,128)(2,1)} fusion(f32[16,4,4096]{2,1,0:T(4,128)} %collective-permute-done.1, f32[16,8,4096]{2,1,0:T(8,128)} %fusion, pred[]{:T(512)S(6)} %eq.103), kind=kLoop, calls=%fused_computation.31 | loop fusion | flops 786432 | bytes 3670017 | tf_op jit(solution)/shard_map/convert_element_type | solution.py:179
  83.9 4.2 %all-to-all-start.2 = ((bf16[16,4,4096]{2,1,0:T(4,128)(2,1)}), bf16[16,4,4096]{2,1,0:T(4,128)(2,1)}, u32[]{:S(2)}, u32[]{:S(2)}) async-start(bf16[16,4,4096]{2,1,0:T(4,128)(2,1)} %add_convert_fusion), calls=%async_computation.2 | async-start | bytes 1048576 | tf_op jit(solution)/shard_map/all_to_all | solution.py:180
  88.2 0.2 fusion.57
  88.4 0.2 select_reduce_fusion
  88.6 0.1 reduce_max.29
  88.7 0.2 fusion.64
  88.9 0.1 fusion.63
  89.0 13.5 %all-to-all-done.2 = bf16[16,4,4096]{2,1,0:T(4,128)(2,1)} async-done(((bf16[16,4,4096]{2,1,0:T(4,128)(2,1)}), bf16[16,4,4096]{2,1,0:T(4,128)(2,1)}, u32[]{:S(2)}, u32[]{:S(2)}) %all-to-all-start.2) | async-done | bytes 524320 | tf_op jit(solution)/shard_map/all_to_all | solution.py:180
  102.5 2.0 %reshape.375 = bf16[64,4096]{1,0:T(8,128)(2,1)} reshape(bf16[16,4,4096]{2,1,0:T(4,128)(2,1)} %all-to-all-done.2) | data formatting | bytes 1048576 | tf_op jit(solution)/shard_map/reshape | solution.py:181
  104.5 3.3 %gather_fusion.3 = bf16[64,4096]{1,0:T(8,128)(2,1)} fusion(bf16[64,4096]{1,0:T(8,128)(2,1)} %reshape.375, s32[1024]{0:T(1024)S(1)} %pad_clamp_fusion), kind=kCustom, calls=%fused_computation.3 | custom fusion | bytes 1048832 | tf_op jit(solution)/shard_map/jit(_take)/gather | solution.py:182
  107.7 1.5 %multiply_reduce_fusion = f32[8,4096]{1,0:T(8,128)S(1)} fusion(bf16[64,4096]{1,0:T(8,128)(2,1)} %gather_fusion.3, f32[8,8]{1,0:T(8,128)S(1)} %fusion.63, pred[8,8]{1,0:T(8,128)(4,1)S(1)} %get-tuple-element.5), kind=kLoop, calls=%fused_computation.30 | loop fusion | flops 1015808 | bytes 655680 | tf_op jit(solution)/shard_map/reduce_sum | solution.py:183
  109.2 0.6 fusion.40
  (47 shorter events, 0.3 us)
Async XLA Ops:
  0.0 67.8 %copy-start = (bf16[1,384,4096]{2,1,0:T(8,128)(2,1)S(1)}, bf16[1,384,4096]{2,1,0:T(8,128)(2,1)}, u32[]{:S(2)}) copy-start(bf16[1,384,4096]{2,1,0:T(8,128)(2,1)} %param.28) | copy-start | bytes 9437188
  2.0 11.9 %copy-start.7 = (s32[8,16]{1,0:T(8,128)S(1)}, s32[8,16]{1,0:T(8,128)}, u32[]{:S(2)}) copy-start(s32[8,16]{1,0:T(8,128)} %param.19) | copy-start | bytes 1540
  6.4 23.8 %all-to-all-start = ((bf16[2,16,2,16,256]{4,3,0,2,1:T(8,128)(2,1)}), bf16[2,16,2,16,256]{4,3,0,2,1:T(8,128)(2,1)}, u32[]{:S(2)}, u32[]{:S(2)}) async-start(bf16[2,16,2,16,256]{4,3,0,2,1:T(8,128)(2,1)} %copy.48), calls=%async_computation | async-start | bytes 1048576 | tf_op jit(solution)/shard_map/all_to_all | solution.py:108
  20.2 4.4 %copy-start.4 = (bf16[8,2,256]{2,1,0:T(2,128)(2,1)S(1)}, bf16[8,2,256]{2,1,0:T(2,128)(2,1)}, u32[]{:S(2)}) copy-start(bf16[8,2,256]{2,1,0:T(2,128)(2,1)} %param.17) | copy-start | bytes 24580
  20.2 4.4 %copy-start.8 = (s32[8]{0:T(128)S(1)}, s32[8]{0:T(128)}, u32[]{:S(2)}) copy-start(s32[8]{0:T(128)} %param.20) | copy-start | bytes 100
  20.2 4.5 %copy-start.6 = (bf16[8,4096]{1,0:T(8,128)(2,1)S(1)}, bf16[8,4096]{1,0:T(8,128)(2,1)}, u32[]{:S(2)}) copy-start(bf16[8,4096]{1,0:T(8,128)(2,1)} %param.16) | copy-start | bytes 196612
  24.6 2.3 %copy-start.2 = (bf16[8,256,2,128]{3,2,1,0:T(2,128)(2,1)S(1)}, bf16[8,256,2,128]{3,2,1,0:T(2,128)(2,1)}, u32[]{:S(2)}) copy-start(bf16[8,256,2,128]{3,2,1,0:T(2,128)(2,1)} %reshape_reshape_squeeze.15) | copy-start | bytes 3145732
  24.8 2.4 %copy-start.3 = (s32[8,8]{1,0:T(8,128)S(1)}, s32[8,8]{1,0:T(8,128)}, u32[]{:S(2)}) copy-start(s32[8,8]{1,0:T(8,128)} %param.29) | copy-start | bytes 772
  26.6 2.1 %copy-start.1 = (s32[16]{0:T(128)S(1)}, s32[16]{0:T(128)}, u32[]{:S(2)}) copy-start(s32[16]{0:T(128)} %param.23) | copy-start | bytes 196
  30.2 8.0 %copy-start.5 = (f32[4096]{0:T(1024)S(1)}, f32[4096]{0:T(1024)}, u32[]{:S(2)}) copy-start(f32[4096]{0:T(1024)} %param.24) | copy-start | bytes 49156
  61.7 2.3 %collective-permute-start = (bf16[16,4,4096]{2,1,0:T(4,128)(2,1)}, bf16[16,4,4096]{2,1,0:T(4,128)(2,1)}, u32[]{:S(2)}, u32[]{:S(2)}) collective-permute-start(bf16[16,4,4096]{2,1,0:T(4,128)(2,1)} %all_to_all.15), channel_id=1, source_target_pairs={{0,1},{1,0},{2,3},{3,2},{4,5},{5,4},{6,7},{7,6},{8,9},{9,8},{10,11... | collective-permute-start | bytes 1572872 | tf_op jit(solution)/shard_map/ppermute | solution.py:23
  77.2 3.0 %collective-permute-start.1 = (f32[16,4,4096]{2,1,0:T(4,128)}, f32[16,4,4096]{2,1,0:T(4,128)}, u32[]{:S(2)}, u32[]{:S(2)}) collective-permute-start(f32[16,4,4096]{2,1,0:T(4,128)} %slice_select_fusion), channel_id=1, source_target_pairs={{0,1},{1,0},{2,3},{3,2},{4,5},{5,4},{6,7},{7,6},{8,9},{9,8},{10,11... | collective-permute-start | bytes 3145736 | tf_op jit(solution)/shard_map/ppermute | solution.py:23
  77.4 10.8 %copy-start.9 = (bf16[4096,8]{0,1:T(8,128)(2,1)S(1)}, bf16[4096,8]{0,1:T(8,128)(2,1)}, u32[]{:S(2)}) copy-start(bf16[4096,8]{0,1:T(8,128)(2,1)} %param.25) | copy-start | bytes 196612
  83.9 18.6 %all-to-all-start.2 = ((bf16[16,4,4096]{2,1,0:T(4,128)(2,1)}), bf16[16,4,4096]{2,1,0:T(4,128)(2,1)}, u32[]{:S(2)}, u32[]{:S(2)}) async-start(bf16[16,4,4096]{2,1,0:T(4,128)(2,1)} %add_convert_fusion), calls=%async_computation.2 | async-start | bytes 1048576 | tf_op jit(solution)/shard_map/all_to_all | solution.py:180
where the time goes:
time: 111 us; the launch traced here: 110 us
  local copies, waits for them, and re-layouts  26.4 us (24%)
  blocking collectives  20.3 us (18%)
  waiting for transfers between devices  18.4 us (17%)
  other arithmetic  16.7 us (15%)
  matrix products  15.7 us (14%)
  starting transfers between devices  12 us (11%)
    all_to_all x1, blocking collectives, local(): lax.all_to_all(outgoing_half, 'expert', split_axis=0, concat_axis=0, tile...  20.3 us
    all_to_all x1, waiting for transfers between devices, local(): lax.all_to_all(finished, 'expert', split_axis=0, concat_axis=0, tiled=True)  13.5 us
    all_to_all x1, starting transfers between devices, local(): lax.all_to_all(outgoing, 'expert', split_axis=1, concat_axis=1, tiled=True)  7.46 us
    dot_general x1, matrix products, local(): jnp.dot(activated, w_down[0], preferred_element_type=jnp.float32)  5.82 us
    ppermute x2, waiting for transfers between devices, partner(): lax.ppermute(x, axis, [(i, i ^ 1 << apart) for i in range(lax.axis_size(a...  4.88 us
    all_to_all x1, starting transfers between devices, local(): lax.all_to_all(finished, 'expert', split_axis=0, concat_axis=0, tiled=True)  4.25 us
    dot_general x1, matrix products, local(): jnp.dot(flattened, w_gate[0], preferred_element_type=jnp.float32)  3.83 us
    convert_element_type x1, other arithmetic, local(): finished = (kept + partner_part).astype(jnp.bfloat16)  3.76 us
  transfers between devices with their start and end apart: 4, of which 3 were waited for; matrix products, arithmetic and copies ran while one was open for 15% of the time, Pallas kernels for 0%

commit v1 on v0

--- a/solution.py
+++ b/solution.py
@@ -1,8 +1,11 @@
+import functools
 import math
 
 import jax
 import jax.numpy as jnp
 from jax import lax
+from jax.experimental import pallas as pl
+from jax.experimental.pallas import tpu as pltpu
 from jax.sharding import PartitionSpec as P
 
 D = 4096
@@ -63,7 +66,7 @@
     return blended_noise.reshape(decode_tokens, QUERY_HEADS * HEAD_SIZE).astype(jnp.bfloat16)
 
 
-def local(
+def routed(
     hidden_in,
     queries,
     decode_key_value,
@@ -184,6 +187,452 @@
     return (resid_wide + expert_mix).astype(jnp.bfloat16)
 
 
+def layer_kernel(
+    devices,
+    picks,
+    hidden_ref,
+    q_ref,
+    dkv_ref,
+    kv_ref,
+    table_ref,
+    blocks_ref,
+    pages_ref,
+    lengths_ref,
+    new_ref,
+    gain_ref,
+    router_ref,
+    count_ref,
+    gate_hbm,
+    up_hbm,
+    down_hbm,
+    out_ref,
+    w_gate,
+    w_up,
+    w_down,
+    kv_send,
+    kv_recv,
+    attn,
+    x_all,
+    gates,
+    part,
+    core_recv,
+    y_send,
+    y_recv,
+    z_send,
+    z_recv,
+    kept,
+    w_sem,
+    kv_ssem,
+    kv_rsem,
+    x_ssem,
+    x_rsem,
+    g_ssem,
+    g_rsem,
+    c_sem,
+    y_sem,
+    zs_sem,
+    zr_sem,
+):
+    f32, bf16 = jnp.float32, jnp.bfloat16
+    me = lax.axis_index("expert")
+    lines = devices // 4
+    core, row, line = lax.rem(me, 2), lax.rem(me // 2, 2), me // 4
+    seqs = hidden_ref.shape[0]
+    group = QUERY_HEADS // KEY_VALUE_HEADS
+    scale = 1.0 / math.sqrt(HEAD_SIZE)
+
+    def device(at_line, at_row, at_core):
+        return (at_line * 2 + at_row) * 2 + at_core
+
+    def place(at_line, at_row, at_core):
+        return (at_core * 2 + at_row) * lines + at_line
+
+    def remote(src, dst, ssem, rsem, to):
+        return pltpu.make_async_remote_copy(
+            src_ref=src,
+            dst_ref=dst,
+            send_sem=ssem,
+            recv_sem=rsem,
+            device_id={"expert": to},
+            device_id_type=pl.DeviceIdType.MESH,
+        )
+
+    weights = [
+        pltpu.make_async_copy(a.at[0], b, w_sem.at[i])
+        for i, (a, b) in enumerate(((gate_hbm, w_gate), (up_hbm, w_up), (down_hbm, w_down)))
+    ]
+    for copy in weights:
+        copy.start()
+
+    barrier = pltpu.get_barrier_semaphore()
+
+    def greet(k, carry):
+        pl.semaphore_signal(
+            barrier,
+            inc=1,
+            device_id={"expert": lax.rem(me + k, devices)},
+            device_id_type=pl.DeviceIdType.MESH,
+        )
+        return carry
+
+    lax.fori_loop(1, devices, greet, 0)
+
+    def stage(o, carry):
+        for r in range(MAXP):
+            kv_send[o, r] = pages_ref[picks[o * MAXP + r]]
+        return carry
+
+    lax.fori_loop(0, devices, stage, 0)
+    for r in range(MAXP):
+        kv_recv[me, r] = pages_ref[picks[me * MAXP + r]]
+    pl.semaphore_wait(barrier, devices - 1)
+
+    def kv_copy(k):
+        to = lax.rem(me + k, devices)
+        return remote(kv_send.at[to], kv_recv.at[me], kv_ssem.at[k], kv_rsem.at[k], to)
+
+    def kv_go(k, carry):
+        kv_copy(k).start()
+        return carry
+
+    lax.fori_loop(1, devices, kv_go, 0)
+
+    tokens = kv_ref.shape[0] * PAGE_TOKENS
+    page_of = lax.broadcasted_iota(jnp.int32, (seqs, tokens), 1) // PAGE_TOKENS
+    held = jnp.zeros((seqs, tokens), f32)
+    for b in range(table_ref.shape[1]):
+        hit = (page_of == table_ref[:, b : b + 1]) & (blocks_ref[:, 0:1] > b)
+        held = held + jnp.where(hit, 1.0, 0.0)
+    held = jnp.concatenate([held] * group, 0)
+
+    def heads(h):
+        rows = q_ref[...].astype(f32)
+        return jnp.concatenate(
+            [rows[:, (h * group + g) * HEAD_SIZE : (h * group + g + 1) * HEAD_SIZE] for g in range(group)],
+            0,
+        )
+
+    def own(h, at):
+        begin = at * KEY_VALUE_HEADS * HEAD_SIZE + h * HEAD_SIZE
+        return jnp.concatenate([dkv_ref[:, begin : begin + HEAD_SIZE].astype(f32)] * group, 0)
+
+    def weigh(scores, times, own_score):
+        scores = jnp.where(times > 0, scores, masked_score)
+        peak = jnp.maximum(jnp.max(scores, -1, keepdims=True), own_score)
+        weight = times * jnp.exp(scores - peak)
+        own_weight = jnp.exp(own_score - peak)
+        total = jnp.sum(weight, -1, keepdims=True) + own_weight
+        return (weight / total).astype(bf16), (own_weight / total).astype(bf16).astype(f32)
+
+    def dot_t(a, b):
+        return lax.dot_general(a, b, (((1,), (1,)), ((), ())), preferred_element_type=f32)
+
+    def spread(h, mixed, old):
+        for g in range(group):
+            at = slice((h * group + g) * HEAD_SIZE, (h * group + g + 1) * HEAD_SIZE)
+            rows = mixed[g * seqs : (g + 1) * seqs]
+            if old:
+                attn[:, at] = rows
+            else:
+                attn[:, at] = jnp.where(new_ref[:, 0:1] > 0, rows, attn[:, at])
+
+    own_scores = []
+    for h in range(KEY_VALUE_HEADS):
+        at = slice(h * HEAD_SIZE, (h + 1) * HEAD_SIZE)
+        queries = heads(h)
+        own_score = jnp.sum(queries * own(h, 0), -1, keepdims=True) * scale
+        own_scores.append(own_score)
+        keys = kv_ref[:, 0, :, at].reshape(tokens, HEAD_SIZE)
+        values = kv_ref[:, 1, :, at].reshape(tokens, HEAD_SIZE)
+        probs, own_prob = weigh(dot_t(queries.astype(bf16), keys) * scale, held, own_score)
+        mixed = jnp.dot(probs, values, preferred_element_type=f32) + own_prob * own(h, 1)
+        spread(h, mixed, True)
+
+    def kv_end(k, carry):
+        kv_copy(k).wait()
+        return carry
+
+    lax.fori_loop(1, devices, kv_end, 0)
+
+    fresh = devices * PAGE_TOKENS
+    slot = lax.rem(lax.broadcasted_iota(jnp.int32, (seqs * group, 1), 0), seqs)
+    ahead = lax.broadcasted_iota(jnp.int32, (seqs, fresh), 1) // PAGE_TOKENS < lengths_ref[:, 0:1]
+    allowed = jnp.concatenate([jnp.where(ahead, 1.0, 0.0)] * group, 0)
+    for h in range(KEY_VALUE_HEADS):
+        at = slice(h * HEAD_SIZE, (h + 1) * HEAD_SIZE)
+        queries = heads(h).astype(bf16)
+        scores = jnp.zeros((seqs * group, fresh), f32)
+        for r in range(MAXP):
+            keys = kv_recv[:, r, 0, :, at].reshape(fresh, HEAD_SIZE)
+            scores = jnp.where(slot == r, dot_t(queries, keys), scores)
+        probs, own_prob = weigh(scores * scale, allowed, own_scores[h])
+        mixed = jnp.zeros((seqs * group, HEAD_SIZE), f32)
+        for r in range(MAXP):
+            values = kv_recv[:, r, 1, :, at].reshape(fresh, HEAD_SIZE)
+            mixed = jnp.where(
+                slot == r, jnp.dot(probs, values, preferred_element_type=f32), mixed
+            )
+        spread(h, mixed + own_prob * own(h, 1), False)
+
+    attention = attn[...].astype(bf16).astype(f32)
+    wide = (hidden_ref[...].astype(f32) + attention).astype(bf16).astype(f32)
+    attn[...] = wide
+    mean = jnp.mean(wide * wide, -1, keepdims=True)
+    normed = (wide * lax.rsqrt(mean + norm_eps) * gain_ref[...]).astype(bf16)
+    mine = place(line, row, core)
+    x_all[mine] = normed
+
+    other_row = device(line, 1 - row, core)
+    other_core = device(line, row, 1 - core)
+
+    def pass_on(buffer, ssem, rsem, spot, at, to):
+        return remote(buffer.at[spot], buffer.at[spot], ssem.at[at], rsem.at[spot], to)
+
+    def first_hops(buffer, ssem, rsem):
+        copies = [
+            pass_on(buffer, ssem, rsem, mine, k, device(lax.rem(line + k, lines), row, core))
+            for k in range(1, lines)
+        ]
+        copies.append(pass_on(buffer, ssem, rsem, mine, 0, other_row))
+        copies.append(pass_on(buffer, ssem, rsem, mine, lines, other_core))
+        for copy in copies:
+            copy.start()
+        return copies
+
+    def arrived(buffer, ssem, rsem, spot):
+        pass_on(buffer, ssem, rsem, spot, 0, other_core).wait_recv()
+
+    pools = ((x_all, x_ssem, x_rsem), (gates, g_ssem, g_rsem))
+    sent = first_hops(*pools[0])
+
+    logits = jnp.dot(normed, router_ref[...], preferred_element_type=f32)
+    times = count_ref[...]
+    picked = jnp.where(times > 0, logits, masked_score)
+    gate = times * jnp.exp(picked - jnp.max(picked, -1, keepdims=True))
+    gate = gate / jnp.sum(gate, -1, keepdims=True)
+    experts = gate.shape[1]
+    gates[mine] = jnp.concatenate([gate] * (128 // experts), 1)
+    sent += first_hops(*pools[1])
+
+    for k in range(1, lines):
+        spot = place(lax.rem(line + k, lines), row, core)
+        for pool in pools:
+            arrived(*pool, spot)
+            for step, to in ((0, other_row), (1, other_core)):
+                copy = pass_on(*pool, spot, lines + 2 * k - 1 + step, to)
+                copy.start()
+                sent.append(copy)
+    for k in range(lines):
+        spot = place(lax.rem(line + k, lines), 1 - row, core)
+        for pool in pools:
+            arrived(*pool, spot)
+            copy = pass_on(*pool, spot, 3 * lines - 1 + k, other_core)
+            copy.start()
+            sent.append(copy)
+    for at_row in range(2):
+        for k in range(lines):
+            for pool in pools:
+                arrived(*pool, place(k, at_row, 1 - core))
+
+    weights[0].wait()
+    weights[1].wait()
+    total = devices * seqs
+    hidden = w_gate.shape[1]
+    step = min(512, D)
+
+    def project(i, carry):
+        at = pl.ds(pl.multiple_of(i * step, step), step)
+        x = x_all[:, :, at].reshape(total, step)
+        return (
+            carry[0] + jnp.dot(x, w_gate[at, :], preferred_element_type=f32),
+            carry[1] + jnp.dot(x, w_up[at, :], preferred_element_type=f32),
+        )
+
+    zeros = jnp.zeros((total, hidden), f32)
+    gate_proj, up_proj = lax.fori_loop(0, D // step, project, (zeros, zeros))
+    lanes = lax.broadcasted_iota(jnp.int32, (total, 128), 1)
+    scaled = jnp.sum(
+        jnp.where(lanes == me // 2, gates[...].reshape(total, 128), 0.0), -1, keepdims=True
+    )
+    activated = (gate_proj / (1.0 + jnp.exp(-gate_proj)) * up_proj * scaled).astype(bf16)
+
+    weights[2].wait()
+    chunks = c_sem.shape[1]
+    width = D // chunks
+
+    def cut(i):
+        return slice(i * width, (i + 1) * width)
+
+    def core_copy(i):
+        return remote(
+            part.at[1 - core, :, :, :, cut(i)],
+            core_recv.at[:, :, :, cut(i)],
+            c_sem.at[0, i],
+            c_sem.at[1, i],
+            other_core,
+        )
+
+    def row_copy(i):
+        return remote(
+            y_send.at[:, :, cut(i)],
+            y_recv.at[:, :, cut(i)],
+            y_sem.at[0, i],
+            y_sem.at[1, i],
+            other_row,
+        )
+
+    def line_copy(i, k):
+        to = lax.rem(line + k, lines)
+        return remote(
+            z_send.at[k, :, cut(i)],
+            z_recv.at[k, :, cut(i)],
+            zs_sem.at[k, i],
+            zr_sem.at[k, i],
+            device(to, row, core),
+        )
+
+    for i in range(chunks):
+        rows = jnp.dot(activated, w_down[:, cut(i)], preferred_element_type=f32)
+        part[:, :, :, :, cut(i)] = rows.astype(bf16).reshape(2, 2, lines, seqs, width)
+        core_copy(i).start()
+    for i in range(chunks):
+        core_copy(i).wait()
+        y_send[:, :, cut(i)] = (
+            part[core, 1 - row, :, :, cut(i)].astype(f32)
+            + core_recv[1 - row, :, :, cut(i)].astype(f32)
+        ).astype(bf16)
+        row_copy(i).start()
+    for i in range(chunks):
+        row_copy(i).wait()
+
+        def summed(at_line):
+            return (
+                part[core, row, at_line, :, cut(i)].astype(f32)
+                + core_recv[row, at_line, :, cut(i)].astype(f32)
+                + y_recv[at_line, :, cut(i)].astype(f32)
+            )
+
+        for k in range(1, lines):
+            z_send[k, :, cut(i)] = summed(lax.rem(line + k, lines)).astype(bf16)
+            line_copy(i, k).start()
+        kept[:, cut(i)] = attn[:, cut(i)] + summed(line)
+    for i in range(chunks):
+        answer = kept[:, cut(i)]
+        for k in range(1, lines):
+            line_copy(i, k).wait()
+            answer = answer + z_recv[k, :, cut(i)].astype(f32)
+        out_ref[:, cut(i)] = answer.astype(bf16)
+    for copy in sent:
+        copy.wait_send()
+
+
+def dense(
+    hidden_in,
+    queries,
+    decode_key_value,
+    local_kv,
+    page_table,
+    seq_blocks,
+    prompt_kv,
+    prompt_owner,
+    prompt_pages,
+    norm_gain,
+    router,
+    w_gate,
+    w_up,
+    w_down,
+    route_ids,
+):
+    devices = lax.axis_size("expert")
+    position = lax.axis_index("expert")
+    experts = router.shape[1]
+    seqs = hidden_in.shape[0]
+    hidden = w_gate.shape[2]
+    lines = devices // 4
+    bf16, f32 = jnp.bfloat16, jnp.float32
+    prompt_range = jnp.arange(prompt_owner.shape[0], dtype=jnp.int32)
+    same_owner = prompt_owner[:, None] == prompt_owner[None, :]
+    earlier = prompt_range[None, :] < prompt_range[:, None]
+    arrival = jnp.sum((same_owner & earlier).astype(jnp.int32), 1)
+    pair = prompt_owner * MAXP + arrival
+    slots = jnp.arange(devices * MAXP, dtype=jnp.int32)
+    picks = jnp.sum(jnp.where(pair[None, :] == slots[:, None], prompt_range[None, :], 0), 1)
+    slot = jnp.arange(seqs, dtype=jnp.int32)
+    here = (prompt_owner[None, :] == position) & (arrival[None, :] == slot[:, None])
+    lengths = jnp.sum(jnp.where(here, prompt_pages[None, :], 0), 1, keepdims=True)
+    is_new = jnp.any(here, 1, keepdims=True).astype(jnp.int32)
+    ids = jnp.arange(experts, dtype=jnp.int32)
+    counts = jnp.sum((route_ids[:, :, None] == ids[None, None, :]).astype(f32), 1)
+    chunks = 4
+    smem = pl.BlockSpec(memory_space=pltpu.SMEM)
+    vmem = pl.BlockSpec(memory_space=pltpu.VMEM)
+    hbm = pl.BlockSpec(memory_space=pl.ANY)
+    dma = pltpu.SemaphoreType.DMA
+    page = (MAXP, 2, PAGE_TOKENS, KEY_VALUE_HEADS * HEAD_SIZE)
+    return pl.pallas_call(
+        functools.partial(layer_kernel, devices),
+        out_shape=jax.ShapeDtypeStruct((seqs, D), bf16),
+        in_specs=[smem] + [vmem] * 12 + [hbm] * 3,
+        out_specs=vmem,
+        scratch_shapes=[
+            pltpu.VMEM((D, hidden), bf16),
+            pltpu.VMEM((D, hidden), bf16),
+            pltpu.VMEM((hidden, D), bf16),
+            pltpu.VMEM((devices,) + page, bf16),
+            pltpu.VMEM((devices,) + page, bf16),
+            pltpu.VMEM((seqs, D), f32),
+            pltpu.VMEM((devices, seqs, D), bf16),
+            pltpu.VMEM((devices, seqs, 128), f32),
+            pltpu.VMEM((2, 2, lines, seqs, D), bf16),
+            pltpu.VMEM((2, lines, seqs, D), bf16),
+            pltpu.VMEM((lines, seqs, D), bf16),
+            pltpu.VMEM((lines, seqs, D), bf16),
+            pltpu.VMEM((lines, seqs, D), bf16),
+            pltpu.VMEM((lines, seqs, D), bf16),
+            pltpu.VMEM((seqs, D), f32),
+            dma((3,)),
+            dma((devices,)),
+            dma((devices,)),
+            dma((4 * lines,)),
+            dma((devices,)),
+            dma((4 * lines,)),
+            dma((devices,)),
+            dma((2, chunks)),
+            dma((2, chunks)),
+            dma((lines, chunks)),
+            dma((lines, chunks)),
+        ],
+        compiler_params=pltpu.CompilerParams(
+            collective_id=0, has_side_effects=True, vmem_limit_bytes=48 << 20
+        ),
+    )(
+        picks,
+        hidden_in,
+        queries,
+        decode_key_value.reshape(seqs, -1),
+        local_kv,
+        page_table,
+        seq_blocks[:, None],
+        prompt_kv[0],
+        lengths,
+        is_new,
+        norm_gain[None, :],
+        router,
+        counts,
+        w_gate,
+        w_up,
+        w_down,
+    )
+
+
+def local(*arrays):
+    devices = lax.axis_size("expert")
+    experts = arrays[10].shape[1]
+    if experts == TOPK and devices == 2 * experts and devices % 4 == 0:
+        return dense(*arrays)
+    return routed(*arrays)
+
+
 def solution(mesh):
     return jax.shard_map(
         local,

time: 111 us -> 65.3 us (0.59)
  Pallas kernels: 0 us -> 50.2 us
  blocking collectives: 20.3 us -> 0 us
  waiting for transfers between devices: 18.4 us -> 0 us
  local copies, waits for them, and re-layouts: 26.4 us -> 10.5 us
  matrix products: 15.7 us -> 0 us
  other arithmetic: 16.7 us -> 3.99 us
  starting transfers between devices: 12 us -> 0 us
    pallas_call x0 -> x1, Pallas kernels: none -> 50.2 us  [dense(): pl.pallas_call(functools.partial(layer_kernel, devices), out_shape=jax.Sh...]
    all_to_all x1 -> x0, blocking collectives: 20.3 us -> none  [local(): lax.all_to_all(outgoing_half, 'expert', split_axis=0, concat_axis=0, tile...]
    dot_general x10 -> x0, matrix products: 15.7 us -> none  [the longest x1 5.82 us: local(): jnp.dot(activated, w_down[0], preferred_element_type=jnp.float32)]
    all_to_all x2 -> x0, waiting for transfers between devices: 13.5 us -> none  [the longest x1 13.5 us: local(): lax.all_to_all(finished, 'expert', split_axis=0, concat_axis=0, tiled=True)]
    all_to_all x2 -> x0, starting transfers between devices: 11.7 us -> none  [the longest x1 7.46 us: local(): lax.all_to_all(outgoing, 'expert', split_axis=1, concat_axis=1, tiled=True)]
    gather x4 -> x0, local copies, waits for them, and re-layouts: 9.3 us -> none  [the longest x1 3.27 us: local(): jnp.take(expert_sum, slot_index, axis=0).astype(jnp.float32)]
    unnamed x25 -> x17, local copies, waits for them, and re-layouts: 3.14 us -> 9.6 us
    another operation x4 -> x0, local copies, waits for them, and re-layouts: 5.91 us -> none  [the longest x2 2.97 us: attend(): rows_of_keys.reshape(decode_tokens, -1, KEY_VALUE_HEADS, HEAD_SIZE)]
  transfers between devices with their start and end apart: 4 -> 0, of which waited for: 3 -> 0; matrix products, arithmetic and copies ran while one was open for 15% -> 0% of each run, Pallas kernels for 0% -> 0%
where the time goes in v1:
time: 65.3 us; the launch traced here: 64.7 us
  Pallas kernels  50.2 us (77%)
  local copies, waits for them, and re-layouts  10.5 us (16%)
  other arithmetic  3.99 us (6%)
    pallas_call x1, Pallas kernels, dense(): pl.pallas_call(functools.partial(layer_kernel, devices), out_shape=jax.Sh...  50.2 us
    unnamed x17, local copies, waits for them, and re-layouts  9.6 us

profile of v1, /device:TPU:0, one launch (start us, length us, event | category | flops | bytes accessed | tf_op | source)
XLA Modules:
  0.0 64.7 jit_solution(5712974845984660160)
XLA Ops:
  0.0 0.7 %broadcast_compare_fusion = pred[16]{0:T(512)(128)(4,1)S(1)} fusion(s32[16]{0:T(128)} %param.22, s32[]{:T(128)S(6)} %axis_index.12), kind=kLoop, calls=%fused_computation.13 | loop fusion | flops 16 | bytes 84 | tf_op jit(solution)/shard_map/eq | solution.py:561
  0.7 0.9 %convert_reduce_fusion.1 = s32[16]{0:T(128)S(1)} fusion(s32[16]{0:T(128)} %param.22), kind=kLoop, calls=%fused_computation.4 | loop fusion | flops 1264 | bytes 128 | tf_op jit(solution)/shard_map/reduce_sum | solution.py:556
  1.6 0.1 fusion.2
  1.7 0.8 %select_reduce_fusion.1 = s32[8]{0:T(128)S(1)} fusion(s32[16]{0:T(128)} %param.23, s32[16]{0:T(128)S(1)} %convert_reduce_fusion.1, pred[16]{0:T(512)(128)(4,1)S(1)} %broadcast_compare_fusion), kind=kLoop, calls=%fused_computation.7 | loop fusion | flops 504 | bytes 176 | tf_op jit(solution)/shard_map/reduce_sum | solution.py:562
  2.5 0.7 %multiply_add_fusion = s32[16]{0:T(128)S(1)} fusion(s32[16]{0:T(128)S(1)} %convert_reduce_fusion.1, s32[16]{0:T(128)} %param.22), kind=kLoop, calls=%fused_computation.12 | loop fusion | flops 32 | bytes 192 | tf_op jit(solution)/shard_map/add | solution.py:557
  3.1 0.1 select_reduce_fusion.picks
  3.2 0.1 copy.22.new_ref
  3.3 0.1 copy.21.lengths_ref
  3.4 0.7 %copy.20.blocks_ref = s32[8,1]{1,0:T(8,128)S(1)} copy(s32[8,1]{0,1:T(1,128)} %bitcast.13) | data formatting | bytes 64 | tf_op jit(solution)/shard_map/broadcast_in_dim | solution.py:615
  4.1 0.8 %convert_reduce_fusion.count_ref = f32[8,8]{1,0:T(8,128)S(1)} fusion(s32[8,8]{1,0:T(8,128)} %param.29), kind=kLoop, calls=%fused_computation | loop fusion | flops 1472 | bytes 512 | tf_op jit(solution)/shard_map/reduce_sum | solution.py:565
  4.9 0.7 %copy.24 = bf16[1,8,2,256]{3,1,2,0:T(8,128)(2,1)S(1)} copy(bf16[1,8,2,256]{3,2,1,0:T(2,128)(2,1)} %bitcast.11) | data formatting | bytes 16384
  5.6 1.3 %copy.23.router_ref = bf16[4096,8]{1,0:T(8,128)(2,1)S(1)} copy(bf16[4096,8]{0,1:T(8,128)(2,1)} %param.25) | data formatting | bytes 131072 | tf_op args[10]
  6.9 0.0 copy-start
  6.9 1.9 %copy-done = bf16[1,4096,384]{2,1,0:T(8,128)(2,1)S(1)} copy-done((bf16[1,4096,384]{2,1,0:T(8,128)(2,1)S(1)}, bf16[1,4096,384]{2,1,0:T(8,128)(2,1)}, u32[]{:S(2)}) %copy-start) | copy-done | bytes 3145752
  8.8 0.0 copy-start.1
  8.8 1.0 %copy-done.1 = bf16[32,2,16,256]{3,2,1,0:T(8,128)(2,1)S(1)} copy-done((bf16[32,2,16,256]{3,2,1,0:T(8,128)(2,1)S(1)}, bf16[32,2,16,256]{3,2,1,0:T(8,128)(2,1)}, u32[]{:S(2)}) %copy-start.1) | copy-done | bytes 524312
  9.9 0.0 copy-start.2
  9.9 0.9 %copy-done.2 = bf16[1,16,2,16,256]{4,3,2,1,0:T(8,128)(2,1)S(1)} copy-done((bf16[1,16,2,16,256]{4,3,2,1,0:T(8,128)(2,1)S(1)}, bf16[1,16,2,16,256]{4,3,2,1,0:T(8,128)(2,1)}, u32[]{:S(2)}) %copy-start.2) | copy-done | bytes 262168
  10.8 0.0 copy-start.3
  10.8 0.8 %copy-done.3 = bf16[8,4096]{1,0:T(8,128)(2,1)S(1)} copy-done((bf16[8,4096]{1,0:T(8,128)(2,1)S(1)}, bf16[8,4096]{1,0:T(8,128)(2,1)}, u32[]{:S(2)}) %copy-start.3) | copy-done | bytes 65560
  11.6 0.0 copy-start.4
  11.6 0.8 %copy-done.4 = bf16[8,4096]{1,0:T(8,128)(2,1)S(1)} copy-done((bf16[8,4096]{1,0:T(8,128)(2,1)S(1)}, bf16[8,4096]{1,0:T(8,128)(2,1)}, u32[]{:S(2)}) %copy-start.4) | copy-done | bytes 65560
  12.5 0.0 copy-start.5
  12.5 0.7 %copy-done.5 = f32[4096]{0:T(1024)S(1)} copy-done((f32[4096]{0:T(1024)S(1)}, f32[4096]{0:T(1024)}, u32[]{:S(2)}) %copy-start.5) | copy-done | bytes 16408
  13.2 0.0 copy-start.6
  13.2 0.7 %copy-done.6 = s32[8,16]{1,0:T(8,128)S(1)} copy-done((s32[8,16]{1,0:T(8,128)S(1)}, s32[8,16]{1,0:T(8,128)}, u32[]{:S(2)}) %copy-start.6) | copy-done | bytes 536
  13.9 50.2 %shard_map.145 = bf16[8,4096]{1,0:T(8,128)(2,1)S(1)} custom-call(s32[32]{0:T(128)S(1)} %select_reduce_fusion.picks, bf16[8,4096]{1,0:T(8,128)(2,1)S(1)} %copy-done.3, bf16[8,4096]{1,0:T(8,128)(2,1)S(1)} %copy-done.4, bf16[8,512]{1,0:T(8,128)(2,1)S(1)} %bitcast.9, bf16[32,2,16,256]{3,2,1,0:T(8,128)(2,1)S(1)} %copy-done.1, s32[8,16]{1,0:T(8,128)S(1)} %copy-done.6, ...), custom_call_target="tpu_custom_call" | custom-call | tf_op jit(solution)/shard_map/pallas_call | solution.py:572
  64.1 0.6 copy.26
  (1 shorter events, 0.0 us)
Async XLA Ops:
  6.9 1.9 %copy-start = (bf16[1,4096,384]{2,1,0:T(8,128)(2,1)S(1)}, bf16[1,4096,384]{2,1,0:T(8,128)(2,1)}, u32[]{:S(2)}) copy-start(bf16[1,4096,384]{2,1,0:T(8,128)(2,1)} %gate_hbm.1) | copy-start | bytes 9437188
  8.8 1.0 %copy-start.1 = (bf16[32,2,16,256]{3,2,1,0:T(8,128)(2,1)S(1)}, bf16[32,2,16,256]{3,2,1,0:T(8,128)(2,1)}, u32[]{:S(2)}) copy-start(bf16[32,2,16,256]{3,2,1,0:T(8,128)(2,1)} %kv_ref.1) | copy-start | bytes 1572868
  9.9 0.9 %copy-start.2 = (bf16[1,16,2,16,256]{4,3,2,1,0:T(8,128)(2,1)S(1)}, bf16[1,16,2,16,256]{4,3,2,1,0:T(8,128)(2,1)}, u32[]{:S(2)}) copy-start(bf16[1,16,2,16,256]{4,3,2,1,0:T(8,128)(2,1)} %param.21) | copy-start | bytes 786436
  10.8 0.8 %copy-start.3 = (bf16[8,4096]{1,0:T(8,128)(2,1)S(1)}, bf16[8,4096]{1,0:T(8,128)(2,1)}, u32[]{:S(2)}) copy-start(bf16[8,4096]{1,0:T(8,128)(2,1)} %hidden_ref.1) | copy-start | bytes 196612
  11.6 0.8 %copy-start.4 = (bf16[8,4096]{1,0:T(8,128)(2,1)S(1)}, bf16[8,4096]{1,0:T(8,128)(2,1)}, u32[]{:S(2)}) copy-start(bf16[8,4096]{1,0:T(8,128)(2,1)} %q_ref.1) | copy-start | bytes 196612
  12.5 0.7 %copy-start.5 = (f32[4096]{0:T(1024)S(1)}, f32[4096]{0:T(1024)}, u32[]{:S(2)}) copy-start(f32[4096]{0:T(1024)} %param.24) | copy-start | bytes 49156
  13.2 0.7 %copy-start.6 = (s32[8,16]{1,0:T(8,128)S(1)}, s32[8,16]{1,0:T(8,128)}, u32[]{:S(2)}) copy-start(s32[8,16]{1,0:T(8,128)} %table_ref.1) | copy-start | bytes 1540

commit v2 on v1

--- a/solution.py
+++ b/solution.py
@@ -189,23 +189,31 @@
 
 def layer_kernel(
     devices,
-    picks,
-    hidden_ref,
-    q_ref,
-    dkv_ref,
-    kv_ref,
-    table_ref,
-    blocks_ref,
-    pages_ref,
-    lengths_ref,
-    new_ref,
-    gain_ref,
-    router_ref,
-    count_ref,
+    owners,
+    prompt_lengths,
+    blocks,
+    pages_hbm,
+    q_hbm,
+    dkv_hbm,
+    table_hbm,
+    kv_hbm,
+    hidden_hbm,
+    gain_hbm,
+    router_hbm,
+    ids_hbm,
     gate_hbm,
     up_hbm,
     down_hbm,
     out_ref,
+    pages_ref,
+    q_ref,
+    dkv_ref,
+    table_ref,
+    kv_ref,
+    hidden_ref,
+    gain_ref,
+    router_ref,
+    ids_ref,
     w_gate,
     w_up,
     w_down,
@@ -221,13 +229,12 @@
     z_send,
     z_recv,
     kept,
+    in_sem,
     w_sem,
     kv_ssem,
     kv_rsem,
     x_ssem,
     x_rsem,
-    g_ssem,
-    g_rsem,
     c_sem,
     y_sem,
     zs_sem,
@@ -257,11 +264,27 @@
             device_id_type=pl.DeviceIdType.MESH,
         )
 
+    loads = [
+        pltpu.make_async_copy(a, b, in_sem.at[i])
+        for i, (a, b) in enumerate(
+            (
+                (pages_hbm, pages_ref),
+                (q_hbm, q_ref),
+                (dkv_hbm, dkv_ref),
+                (table_hbm, table_ref),
+                (kv_hbm, kv_ref),
+                (hidden_hbm, hidden_ref),
+                (gain_hbm, gain_ref),
+                (router_hbm, router_ref),
+                (ids_hbm, ids_ref),
+            )
+        )
+    ]
     weights = [
         pltpu.make_async_copy(a.at[0], b, w_sem.at[i])
         for i, (a, b) in enumerate(((gate_hbm, w_gate), (up_hbm, w_up), (down_hbm, w_down)))
     ]
-    for copy in weights:
+    for copy in loads + weights:
         copy.start()
 
     barrier = pltpu.get_barrier_semaphore()
@@ -277,14 +300,29 @@
 
     lax.fori_loop(1, devices, greet, 0)
 
+    prompts = owners.shape[0]
+
+    def named(o):
+        first, last, number = jnp.int32(0), jnp.int32(0), jnp.int32(0)
+        for p in range(prompts):
+            hit = owners[p] == o
+            last = jnp.where(hit, p, last)
+            number = number + hit.astype(jnp.int32)
+        for p in reversed(range(prompts)):
+            first = jnp.where(owners[p] == o, p, first)
+        return (first, last), number
+
     def stage(o, carry):
+        picks, _ = named(o)
         for r in range(MAXP):
-            kv_send[o, r] = pages_ref[picks[o * MAXP + r]]
+            kv_send[o, r] = pages_ref[picks[r]]
         return carry
 
+    loads[0].wait()
     lax.fori_loop(0, devices, stage, 0)
+    own_picks, new_count = named(me)
     for r in range(MAXP):
-        kv_recv[me, r] = pages_ref[picks[me * MAXP + r]]
+        kv_recv[me, r] = pages_ref[own_picks[r]]
     pl.semaphore_wait(barrier, devices - 1)
 
     def kv_copy(k):
@@ -297,24 +335,37 @@
 
     lax.fori_loop(1, devices, kv_go, 0)
 
+    for copy in loads[1:]:
+        copy.wait()
+
+    def per_seq(values, shape):
+        at = lax.broadcasted_iota(jnp.int32, shape, 0)
+        return sum(jnp.where(at == s, v, 0) for s, v in enumerate(values))
+
     tokens = kv_ref.shape[0] * PAGE_TOKENS
+    limit = per_seq([blocks[s] for s in range(seqs)], (seqs, tokens))
     page_of = lax.broadcasted_iota(jnp.int32, (seqs, tokens), 1) // PAGE_TOKENS
     held = jnp.zeros((seqs, tokens), f32)
     for b in range(table_ref.shape[1]):
-        hit = (page_of == table_ref[:, b : b + 1]) & (blocks_ref[:, 0:1] > b)
+        hit = (page_of == table_ref[:, b : b + 1]) & (limit > b)
         held = held + jnp.where(hit, 1.0, 0.0)
     held = jnp.concatenate([held] * group, 0)
 
     def heads(h):
         rows = q_ref[...].astype(f32)
         return jnp.concatenate(
-            [rows[:, (h * group + g) * HEAD_SIZE : (h * group + g + 1) * HEAD_SIZE] for g in range(group)],
+            [
+                rows[:, (h * group + g) * HEAD_SIZE : (h * group + g + 1) * HEAD_SIZE]
+                for g in range(group)
+            ],
             0,
         )
 
     def own(h, at):
-        begin = at * KEY_VALUE_HEADS * HEAD_SIZE + h * HEAD_SIZE
-        return jnp.concatenate([dkv_ref[:, begin : begin + HEAD_SIZE].astype(f32)] * group, 0)
+        both = dkv_ref[...].astype(f32)
+        return jnp.concatenate(
+            [both[:, at, h * HEAD_SIZE : (h + 1) * HEAD_SIZE]] * group, 0
+        )
 
     def weigh(scores, times, own_score):
         scores = jnp.where(times > 0, scores, masked_score)
@@ -334,7 +385,7 @@
             if old:
                 attn[:, at] = rows
             else:
-                attn[:, at] = jnp.where(new_ref[:, 0:1] > 0, rows, attn[:, at])
+                attn[:, at] = jnp.where(is_new, rows, attn[:, at])
 
     own_scores = []
     for h in range(KEY_VALUE_HEADS):
@@ -356,7 +407,9 @@
 
     fresh = devices * PAGE_TOKENS
     slot = lax.rem(lax.broadcasted_iota(jnp.int32, (seqs * group, 1), 0), seqs)
-    ahead = lax.broadcasted_iota(jnp.int32, (seqs, fresh), 1) // PAGE_TOKENS < lengths_ref[:, 0:1]
+    length = per_seq([prompt_lengths[p] for p in own_picks], (seqs, fresh))
+    ahead = lax.broadcasted_iota(jnp.int32, (seqs, fresh), 1) // PAGE_TOKENS < length
+    is_new = lax.broadcasted_iota(jnp.int32, (seqs, HEAD_SIZE), 0) < new_count
     allowed = jnp.concatenate([jnp.where(ahead, 1.0, 0.0)] * group, 0)
     for h in range(KEY_VALUE_HEADS):
         at = slice(h * HEAD_SIZE, (h + 1) * HEAD_SIZE)
@@ -385,54 +438,68 @@
     other_row = device(line, 1 - row, core)
     other_core = device(line, row, 1 - core)
 
-    def pass_on(buffer, ssem, rsem, spot, at, to):
-        return remote(buffer.at[spot], buffer.at[spot], ssem.at[at], rsem.at[spot], to)
-
-    def first_hops(buffer, ssem, rsem):
-        copies = [
-            pass_on(buffer, ssem, rsem, mine, k, device(lax.rem(line + k, lines), row, core))
-            for k in range(1, lines)
-        ]
-        copies.append(pass_on(buffer, ssem, rsem, mine, 0, other_row))
-        copies.append(pass_on(buffer, ssem, rsem, mine, lines, other_core))
+    def pass_on(pool, spot, at, to):
+        buffer, cols, n, ssem, rsem = pool
+        ref = buffer.at[spot, :, cols]
+        return remote(ref, ref, ssem.at[n, at], rsem.at[n, spot], to)
+
+    def first_hops(pool):
+        copies = [pass_on(pool, mine, 0, other_row)]
+        for k in range(1, lines):
+            copies.append(pass_on(pool, mine, k, device(lax.rem(line + k, lines), row, core)))
+        copies.append(pass_on(pool, mine, lines, other_core))
         for copy in copies:
             copy.start()
         return copies
 
-    def arrived(buffer, ssem, rsem, spot):
-        pass_on(buffer, ssem, rsem, spot, 0, other_core).wait_recv()
-
-    pools = ((x_all, x_ssem, x_rsem), (gates, g_ssem, g_rsem))
-    sent = first_hops(*pools[0])
-
-    logits = jnp.dot(normed, router_ref[...], preferred_element_type=f32)
-    times = count_ref[...]
+    def arrived(pool, spot):
+        pass_on(pool, spot, 0, other_core).wait_recv()
+
+    pieces = x_rsem.shape[0] - 1
+    piece = D // pieces
+    pools = [
+        (x_all, slice(n * piece, (n + 1) * piece), n, x_ssem, x_rsem) for n in range(pieces)
+    ]
+    sent = []
+    for pool in pools:
+        sent += first_hops(pool)
+
+    logits = dot_t(normed, router_ref[...])
+    experts = logits.shape[1]
+    expert_of = lax.broadcasted_iota(jnp.int32, (seqs, experts), 1)
+    times = jnp.zeros((seqs, experts), f32)
+    for k in range(ids_ref.shape[1]):
+        times = times + jnp.where(ids_ref[:, k : k + 1] == expert_of, 1.0, 0.0)
     picked = jnp.where(times > 0, logits, masked_score)
     gate = times * jnp.exp(picked - jnp.max(picked, -1, keepdims=True))
     gate = gate / jnp.sum(gate, -1, keepdims=True)
-    experts = gate.shape[1]
     gates[mine] = jnp.concatenate([gate] * (128 // experts), 1)
-    sent += first_hops(*pools[1])
-
+    pools.append((gates, slice(0, 128), pieces, x_ssem, x_rsem))
+    sent += first_hops(pools[-1])
+
+    def over_core(k):
+        spot = place(lax.rem(line + k, lines), 1 - row, core)
+        for pool in pools:
+            arrived(pool, spot)
+            copy = pass_on(pool, spot, 3 * lines - 1 + k, other_core)
+            copy.start()
+            sent.append(copy)
+
+    over_core(0)
     for k in range(1, lines):
         spot = place(lax.rem(line + k, lines), row, core)
         for pool in pools:
-            arrived(*pool, spot)
+            arrived(pool, spot)
             for step, to in ((0, other_row), (1, other_core)):
-                copy = pass_on(*pool, spot, lines + 2 * k - 1 + step, to)
+                copy = pass_on(pool, spot, lines + 2 * k - 1 + step, to)
                 copy.start()
                 sent.append(copy)
-    for k in range(lines):
-        spot = place(lax.rem(line + k, lines), 1 - row, core)
-        for pool in pools:
-            arrived(*pool, spot)
-            copy = pass_on(*pool, spot, 3 * lines - 1 + k, other_core)
-            copy.start()
-            sent.append(copy)
+    for k in range(1, lines):
+        over_core(k)
     for at_row in range(2):
         for k in range(lines):
             for pool in pools:
-                arrived(*pool, place(k, at_row, 1 - core))
+                arrived(pool, place(k, at_row, 1 - core))
 
     weights[0].wait()
     weights[1].wait()
@@ -544,37 +611,35 @@
     route_ids,
 ):
     devices = lax.axis_size("expert")
-    position = lax.axis_index("expert")
-    experts = router.shape[1]
     seqs = hidden_in.shape[0]
     hidden = w_gate.shape[2]
     lines = devices // 4
     bf16, f32 = jnp.bfloat16, jnp.float32
-    prompt_range = jnp.arange(prompt_owner.shape[0], dtype=jnp.int32)
-    same_owner = prompt_owner[:, None] == prompt_owner[None, :]
-    earlier = prompt_range[None, :] < prompt_range[:, None]
-    arrival = jnp.sum((same_owner & earlier).astype(jnp.int32), 1)
-    pair = prompt_owner * MAXP + arrival
-    slots = jnp.arange(devices * MAXP, dtype=jnp.int32)
-    picks = jnp.sum(jnp.where(pair[None, :] == slots[:, None], prompt_range[None, :], 0), 1)
-    slot = jnp.arange(seqs, dtype=jnp.int32)
-    here = (prompt_owner[None, :] == position) & (arrival[None, :] == slot[:, None])
-    lengths = jnp.sum(jnp.where(here, prompt_pages[None, :], 0), 1, keepdims=True)
-    is_new = jnp.any(here, 1, keepdims=True).astype(jnp.int32)
-    ids = jnp.arange(experts, dtype=jnp.int32)
-    counts = jnp.sum((route_ids[:, :, None] == ids[None, None, :]).astype(f32), 1)
-    chunks = 4
+    chunks = 8
+    pieces = 2
+    loaded = (
+        prompt_kv[0],
+        queries,
+        decode_key_value,
+        page_table,
+        local_kv,
+        hidden_in,
+        norm_gain[None, :],
+        router.T,
+        route_ids,
+    )
     smem = pl.BlockSpec(memory_space=pltpu.SMEM)
     vmem = pl.BlockSpec(memory_space=pltpu.VMEM)
-    hbm = pl.BlockSpec(memory_space=pl.ANY)
+    hbm = pl.BlockSpec(memory_space=pltpu.HBM)
     dma = pltpu.SemaphoreType.DMA
     page = (MAXP, 2, PAGE_TOKENS, KEY_VALUE_HEADS * HEAD_SIZE)
     return pl.pallas_call(
         functools.partial(layer_kernel, devices),
         out_shape=jax.ShapeDtypeStruct((seqs, D), bf16),
-        in_specs=[smem] + [vmem] * 12 + [hbm] * 3,
+        in_specs=[smem] * 3 + [hbm] * (len(loaded) + 3),
         out_specs=vmem,
-        scratch_shapes=[
+        scratch_shapes=[pltpu.VMEM(a.shape, a.dtype) for a in loaded]
+        + [
             pltpu.VMEM((D, hidden), bf16),
             pltpu.VMEM((D, hidden), bf16),
             pltpu.VMEM((hidden, D), bf16),
@@ -590,39 +655,21 @@
             pltpu.VMEM((lines, seqs, D), bf16),
             pltpu.VMEM((lines, seqs, D), bf16),
             pltpu.VMEM((seqs, D), f32),
+            dma((len(loaded),)),
             dma((3,)),
             dma((devices,)),
             dma((devices,)),
-            dma((4 * lines,)),
-            dma((devices,)),
-            dma((4 * lines,)),
-            dma((devices,)),
+            dma((pieces + 1, 4 * lines)),
+            dma((pieces + 1, devices)),
             dma((2, chunks)),
             dma((2, chunks)),
             dma((lines, chunks)),
             dma((lines, chunks)),
         ],
         compiler_params=pltpu.CompilerParams(
-            collective_id=0, has_side_effects=True, vmem_limit_bytes=48 << 20
+            collective_id=0, has_side_effects=True, vmem_limit_bytes=67043328
         ),
-    )(
-        picks,
-        hidden_in,
-        queries,
-        decode_key_value.reshape(seqs, -1),
-        local_kv,
-        page_table,
-        seq_blocks[:, None],
-        prompt_kv[0],
-        lengths,
-        is_new,
-        norm_gain[None, :],
-        router,
-        counts,
-        w_gate,
-        w_up,
-        w_down,
-    )
+    )(prompt_owner, prompt_pages, seq_blocks, *loaded, w_gate, w_up, w_down)
 
 
 def local(*arrays):

time: 65.3 us -> 52.7 us (0.81)
  local copies, waits for them, and re-layouts: 10.5 us -> 1.47 us
  other arithmetic: 3.99 us -> 0 us
  Pallas kernels: 50.2 us -> 51 us
    unnamed x17 -> x1, local copies, waits for them, and re-layouts: 9.6 us -> 1.47 us
    reduce_sum x4 -> x0, other arithmetic: 2.55 us -> none  [the longest x1 0.91 us: dense(): arrival = jnp.sum((same_owner & earlier).astype(jnp.int32), 1)]
    pallas_call x1, Pallas kernels: 50.2 us -> 51 us  [dense(): pl.pallas_call(functools.partial(layer_kernel, devices), out_shape=jax.Sh...]
    broadcast_in_dim x2 -> x0, local copies, waits for them, and re-layouts: 0.81 us -> none  [the longest x1 0.73 us: dense(): seq_blocks[:, None]]
    add x1 -> x0, other arithmetic: 0.66 us -> none  [dense(): pair = prompt_owner * MAXP + arrival]
    eq x1 -> x0, other arithmetic: 0.66 us -> none  [dense(): prompt_owner[None, :] == position]
where the time goes in v2:
time: 52.7 us; the launch traced here: 52.5 us
  Pallas kernels  51 us (97%)
  local copies, waits for them, and re-layouts  1.47 us (3%)
    pallas_call x1, Pallas kernels, dense(): pl.pallas_call(functools.partial(layer_kernel, devices), out_shape=jax.Sh...  51 us
    unnamed x1, local copies, waits for them, and re-layouts  1.47 us

profile of v2, /device:TPU:0, one launch (start us, length us, event | category | flops | bytes accessed | tf_op | source)
XLA Modules:
  0.0 52.5 jit_solution(8223473205942497928)
XLA Ops:
  0.0 51.0 %shard_map.145 = bf16[8,4096]{1,0:T(8,128)(2,1)} custom-call(s32[16]{0:T(128)} %owners.1, s32[16]{0:T(128)} %prompt_lengths.1, s32[8]{0:T(128)} %blocks.1, bf16[16,2,16,256]{3,2,1,0:T(8,128)(2,1)} %bitcast.3, bf16[8,4096]{1,0:T(8,128)(2,1)} %q_hbm.1, bf16[8,2,256]{2,1,0:T(2,128)(2,1)} %dkv_hbm.1, s32[8,16]{1,0:T(8,128)} %table_hbm.1, ...), custom_call_target="tpu_custom_call" | custom-call | tf_op jit(solution)/shard_map/pallas_call | solution.py:636
  51.1 1.5 %copy.17 = bf16[8,4096]{1,0:T(8,128)(2,1)} copy(bf16[8,4096]{1,0:T(8,128)(2,1)} %shard_map.145) | data formatting | bytes 131072

commit v3 on v2

--- a/solution.py
+++ b/solution.py
@@ -221,6 +221,7 @@
     kv_recv,
     attn,
     x_all,
+    x_new,
     gates,
     part,
     core_recv,
@@ -399,6 +400,45 @@
         mixed = jnp.dot(probs, values, preferred_element_type=f32) + own_prob * own(h, 1)
         spread(h, mixed, True)
 
+    def normalize():
+        attention = attn[...].astype(bf16).astype(f32)
+        wide = (hidden_ref[...].astype(f32) + attention).astype(bf16).astype(f32)
+        mean = jnp.mean(wide * wide, -1, keepdims=True)
+        return wide, (wide * lax.rsqrt(mean + norm_eps) * gain_ref[...]).astype(bf16)
+
+    mine = place(line, row, core)
+    other_row = device(line, 1 - row, core)
+    other_core = device(line, row, 1 - core)
+
+    def pass_on(pool, spot, at, to):
+        buffer, cols, n, ssem, rsem = pool
+        ref = buffer.at[spot, :, cols]
+        return remote(ref, ref, ssem.at[n, at], rsem.at[n, spot], to)
+
+    def first_hops(pool):
+        copies = [pass_on(pool, mine, 0, other_row)]
+        for k in range(1, lines):
+            copies.append(pass_on(pool, mine, k, device(lax.rem(line + k, lines), row, core)))
+        copies.append(pass_on(pool, mine, lines, other_core))
+        for copy in copies:
+            copy.start()
+        return copies
+
+    def arrived(pool, spot):
+        pass_on(pool, spot, 0, other_core).wait_recv()
+
+    pieces = x_rsem.shape[0] - 2
+    piece = D // pieces
+    pools = [
+        (x_all, slice(n * piece, (n + 1) * piece), n, x_ssem, x_rsem) for n in range(pieces)
+    ]
+    x_all[mine] = normalize()[1]
+    sent = []
+    for pool in pools:
+        sent += first_hops(pool)
+    early = tuple(pools)
+    pools.append((x_new, slice(0, D), pieces, x_ssem, x_rsem))
+
     def kv_end(k, carry):
         kv_copy(k).wait()
         return carry
@@ -427,42 +467,10 @@
             )
         spread(h, mixed + own_prob * own(h, 1), False)
 
-    attention = attn[...].astype(bf16).astype(f32)
-    wide = (hidden_ref[...].astype(f32) + attention).astype(bf16).astype(f32)
+    wide, normed = normalize()
     attn[...] = wide
-    mean = jnp.mean(wide * wide, -1, keepdims=True)
-    normed = (wide * lax.rsqrt(mean + norm_eps) * gain_ref[...]).astype(bf16)
-    mine = place(line, row, core)
-    x_all[mine] = normed
-
-    other_row = device(line, 1 - row, core)
-    other_core = device(line, row, 1 - core)
-
-    def pass_on(pool, spot, at, to):
-        buffer, cols, n, ssem, rsem = pool
-        ref = buffer.at[spot, :, cols]
-        return remote(ref, ref, ssem.at[n, at], rsem.at[n, spot], to)
-
-    def first_hops(pool):
-        copies = [pass_on(pool, mine, 0, other_row)]
-        for k in range(1, lines):
-            copies.append(pass_on(pool, mine, k, device(lax.rem(line + k, lines), row, core)))
-        copies.append(pass_on(pool, mine, lines, other_core))
-        for copy in copies:
-            copy.start()
-        return copies
-
-    def arrived(pool, spot):
-        pass_on(pool, spot, 0, other_core).wait_recv()
-
-    pieces = x_rsem.shape[0] - 1
-    piece = D // pieces
-    pools = [
-        (x_all, slice(n * piece, (n + 1) * piece), n, x_ssem, x_rsem) for n in range(pieces)
-    ]
-    sent = []
-    for pool in pools:
-        sent += first_hops(pool)
+    x_new[mine] = normed[:MAXP]
+    sent += first_hops(pools[-1])
 
     logits = dot_t(normed, router_ref[...])
     experts = logits.shape[1]
@@ -474,32 +482,41 @@
     gate = times * jnp.exp(picked - jnp.max(picked, -1, keepdims=True))
     gate = gate / jnp.sum(gate, -1, keepdims=True)
     gates[mine] = jnp.concatenate([gate] * (128 // experts), 1)
-    pools.append((gates, slice(0, 128), pieces, x_ssem, x_rsem))
+    pools.append((gates, slice(0, 128), pieces + 1, x_ssem, x_rsem))
     sent += first_hops(pools[-1])
 
-    def over_core(k):
-        spot = place(lax.rem(line + k, lines), 1 - row, core)
-        for pool in pools:
-            arrived(pool, spot)
-            copy = pass_on(pool, spot, 3 * lines - 1 + k, other_core)
-            copy.start()
-            sent.append(copy)
-
-    over_core(0)
-    for k in range(1, lines):
-        spot = place(lax.rem(line + k, lines), row, core)
-        for pool in pools:
-            arrived(pool, spot)
-            for step, to in ((0, other_row), (1, other_core)):
-                copy = pass_on(pool, spot, lines + 2 * k - 1 + step, to)
+    late = tuple(pools[len(early) :])
+
+    def over_row(group_of):
+        for k in range(1, lines):
+            spot = place(lax.rem(line + k, lines), row, core)
+            for pool in group_of:
+                arrived(pool, spot)
+                for step, to in ((0, other_row), (1, other_core)):
+                    copy = pass_on(pool, spot, lines + 2 * k - 1 + step, to)
+                    copy.start()
+                    sent.append(copy)
+
+    def over_core(group_of):
+        for k in range(lines):
+            spot = place(lax.rem(line + k, lines), 1 - row, core)
+            for pool in group_of:
+                arrived(pool, spot)
+                copy = pass_on(pool, spot, 3 * lines - 1 + k, other_core)
                 copy.start()
                 sent.append(copy)
-    for k in range(1, lines):
-        over_core(k)
-    for at_row in range(2):
-        for k in range(lines):
-            for pool in pools:
-                arrived(pool, place(k, at_row, 1 - core))
+
+    def settle(group_of):
+        for at_row in range(2):
+            for k in range(lines):
+                for pool in group_of:
+                    arrived(pool, place(k, at_row, 1 - core))
+
+    over_row(early)
+    over_row(late)
+    over_core(early)
+    over_core(late)
+    settle(early)
 
     weights[0].wait()
     weights[1].wait()
@@ -507,21 +524,38 @@
     hidden = w_gate.shape[1]
     step = min(512, D)
 
-    def project(i, carry):
-        at = pl.ds(pl.multiple_of(i * step, step), step)
-        x = x_all[:, :, at].reshape(total, step)
-        return (
-            carry[0] + jnp.dot(x, w_gate[at, :], preferred_element_type=f32),
-            carry[1] + jnp.dot(x, w_up[at, :], preferred_element_type=f32),
-        )
-
-    zeros = jnp.zeros((total, hidden), f32)
-    gate_proj, up_proj = lax.fori_loop(0, D // step, project, (zeros, zeros))
+    def activate(rows, read):
+        def project(i, carry):
+            at = pl.ds(pl.multiple_of(i * step, step), step)
+            x = read(at)
+            return (
+                carry[0] + jnp.dot(x, w_gate[at, :], preferred_element_type=f32),
+                carry[1] + jnp.dot(x, w_up[at, :], preferred_element_type=f32),
+            )
+
+        zeros = jnp.zeros((rows, hidden), f32)
+        gate_proj, up_proj = lax.fori_loop(0, D // step, project, (zeros, zeros))
+        return gate_proj / (1.0 + jnp.exp(-gate_proj)) * up_proj
+
+    wait_rows = activate(total, lambda at: x_all[:, :, at].reshape(total, step))
+    settle(late)
+    fresh_rows = activate(
+        devices * MAXP,
+        lambda at: x_new[:, :, at].astype(f32).reshape(devices * MAXP, step).astype(bf16),
+    ).astype(bf16)
+    token = lax.broadcasted_iota(jnp.int32, (total, devices * MAXP), 0)
+    source = lax.broadcasted_iota(jnp.int32, (total, devices * MAXP), 1)
+    moved = (token // seqs == source // MAXP) & (lax.rem(token, seqs) == lax.rem(source, MAXP))
+    replaced = jnp.dot(
+        jnp.where(moved, 1.0, 0.0).astype(bf16), fresh_rows, preferred_element_type=f32
+    )
+    spot_row = lax.rem(lax.broadcasted_iota(jnp.int32, (total, 1), 0), seqs)
+    merged = jnp.where(spot_row < MAXP, replaced, wait_rows)
     lanes = lax.broadcasted_iota(jnp.int32, (total, 128), 1)
     scaled = jnp.sum(
         jnp.where(lanes == me // 2, gates[...].reshape(total, 128), 0.0), -1, keepdims=True
     )
-    activated = (gate_proj / (1.0 + jnp.exp(-gate_proj)) * up_proj * scaled).astype(bf16)
+    activated = (merged * scaled).astype(bf16)
 
     weights[2].wait()
     chunks = c_sem.shape[1]
@@ -616,7 +650,7 @@
     lines = devices // 4
     bf16, f32 = jnp.bfloat16, jnp.float32
     chunks = 8
-    pieces = 2
+    pieces = 1
     loaded = (
         prompt_kv[0],
         queries,
@@ -647,6 +681,7 @@
             pltpu.VMEM((devices,) + page, bf16),
             pltpu.VMEM((seqs, D), f32),
             pltpu.VMEM((devices, seqs, D), bf16),
+            pltpu.VMEM((devices, MAXP, D), bf16),
             pltpu.VMEM((devices, seqs, 128), f32),
             pltpu.VMEM((2, 2, lines, seqs, D), bf16),
             pltpu.VMEM((2, lines, seqs, D), bf16),
@@ -659,8 +694,8 @@
             dma((3,)),
             dma((devices,)),
             dma((devices,)),
-            dma((pieces + 1, 4 * lines)),
-            dma((pieces + 1, devices)),
+            dma((pieces + 2, 4 * lines)),
+            dma((pieces + 2, devices)),
             dma((2, chunks)),
             dma((2, chunks)),
             dma((lines, chunks)),

time: 52.7 us -> 55 us (1.044)
  Pallas kernels: 51 us -> 53.3 us
    pallas_call x1, Pallas kernels: 51 us -> 53.3 us  [dense(): pl.pallas_call(functools.partial(layer_kernel, devices), out_shape=jax.Sh...]
where the time goes in v3:
time: 55 us; the launch traced here: 54.8 us
  Pallas kernels  53.3 us (97%)
  local copies, waits for them, and re-layouts  1.47 us (3%)
    pallas_call x1, Pallas kernels, dense(): pl.pallas_call(functools.partial(layer_kernel, devices), out_shape=jax.Sh...  53.3 us
    unnamed x1, local copies, waits for them, and re-layouts  1.47 us

profile of v3, /device:TPU:0, one launch (start us, length us, event | category | flops | bytes accessed | tf_op | source)
XLA Modules:
  0.0 54.8 jit_solution(4690468384736514059)
XLA Ops:
  0.0 53.3 %shard_map.145 = bf16[8,4096]{1,0:T(8,128)(2,1)} custom-call(s32[16]{0:T(128)} %owners.1, s32[16]{0:T(128)} %prompt_lengths.1, s32[8]{0:T(128)} %blocks.1, bf16[16,2,16,256]{3,2,1,0:T(8,128)(2,1)} %bitcast.3, bf16[8,4096]{1,0:T(8,128)(2,1)} %q_hbm.1, bf16[8,2,256]{2,1,0:T(2,128)(2,1)} %dkv_hbm.1, s32[8,16]{1,0:T(8,128)} %table_hbm.1, ...), custom_call_target="tpu_custom_call" | custom-call | tf_op jit(solution)/shard_map/pallas_call | solution.py:670
  53.3 1.5 %copy.17 = bf16[8,4096]{1,0:T(8,128)(2,1)} copy(bf16[8,4096]{1,0:T(8,128)(2,1)} %shard_map.145) | data formatting | bytes 131072
